TPU v7x, 32 devices: a whole 2x2x4 slice. The times are simulated.
32 devices in a mesh: dp: 8 (over z, y), tensor: 4 (over x, core).
Axes of the slice: x: 2, y: 2, z: 4, core: 2. Of those that a mesh axis runs over, the one named last changes fastest.
Arguments:
- tokens: bfloat16 [16384, 768], P('dp'), may hold values from -6 to 6
- cotangent: bfloat16 [16384, 768], P('dp'), may hold values from -6 to 6
- counts: int32 [16, 5], P('dp'), may hold values from 0 to 576, as said below
- sides: int32 [16, 5], P('dp'), may hold values from 0 to 24, as said below
- segments: int32 [16384], P('dp'), may hold values from 0 to 5, as said below
- norm1_gain: float32 [768], replicated, may hold values from 0.5 to 1.5
- norm1_shift: float32 [768], replicated, may hold values from -3 to 3
- w_qkv: bfloat16 [768, 3, 768], P(None, None, 'tensor'), may hold values from -0.21875 to 0.21875
- b_qkv: float32 [3, 768], P(None, 'tensor'), may hold values from -3 to 3
- freqs: float32 [12, 2, 32], P('tensor'), may hold values from -2 to 2
- w_out: bfloat16 [768, 768], P('tensor'), may hold values from -1.5 to 1.5
- b_out: float32 [768], replicated, may hold values from -3 to 3
- norm2_gain: float32 [768], replicated, may hold values from 0.5 to 1.5
- norm2_shift: float32 [768], replicated, may hold values from -3 to 3
- w_fc1: bfloat16 [768, 3072], P(None, 'tensor'), may hold values from -0.21875 to 0.21875
- b_fc1: float32 [3072], P('tensor'), may hold values from -3 to 3
- w_fc2: bfloat16 [3072, 768], P('tensor'), may hold values from -0.109375 to 0.109375
- b_fc2: float32 [768], replicated, may hold values from -3 to 3
Outputs:
- block_output: bfloat16 [16384, 768], P('dp')
- token_grad: float32 [16384, 768], P('dp')
- norm1_gain_grad: float32 [768], replicated
- norm1_shift_grad: float32 [768], replicated
- qkv_grad: float32 [768, 3, 768], P(None, None, 'tensor')
- qkv_bias_grad: float32 [3, 768], P(None, 'tensor')
- freqs_grad: float32 [12, 2, 32], P('tensor')
- out_grad: float32 [768, 768], P('tensor')
- out_bias_grad: float32 [768], replicated
- norm2_gain_grad: float32 [768], replicated
- norm2_shift_grad: float32 [768], replicated
- fc1_grad: float32 [768, 3072], P(None, 'tensor')
- fc1_bias_grad: float32 [3072], P('tensor')
- fc2_grad: float32 [3072, 768], P('tensor')
- fc2_bias_grad: float32 [768], replicated
Inputs may be any that keep to these rules, and one draw needn't show every extreme that they name: `counts`: A used image slot holds the square of its side; unused slots hold 0 and come after the used ones; a pack's total is under 1024. `sides`: side of each image's square patch grid; 0 for an unused slot. `segments`: each image lies whole in its pack from the pack's first slot on, in slot order and row-major patch order; slots after the last image hold 5 (padding).
All inputs are finite; a program needn't handle non-finite values.
Results may differ from a plain program's by a relative error of at most 0.014.
Values may be sent and summed in bfloat16 or wider, within the bound.
A program may use at most 128 MiB of HBM per device.

v0:
```python
import jax
import jax.numpy as jnp
from jax import lax
from jax.sharding import PartitionSpec as P


def layer_stats(values_in, norm_gain, norm_shift):
    center = values_in - jnp.mean(values_in, axis=-1, keepdims=True)
    inverse = lax.rsqrt(jnp.mean(center * center, axis=-1, keepdims=True) + 1e-06)
    scaled = center * inverse
    return (scaled * norm_gain + norm_shift, scaled, inverse)


def norm_back(grad_normed, scaled, inverse, norm_gain):
    grad_scaled = grad_normed * norm_gain
    return inverse * (
        grad_scaled
        - jnp.mean(grad_scaled, axis=-1, keepdims=True)
        - scaled * jnp.mean(grad_scaled * scaled, axis=-1, keepdims=True)
    )


def positions(segment_ids, image_counts, image_sides):
    slot_count = image_counts.shape[0]
    starts = jnp.cumsum(image_counts, dtype=jnp.int32) - image_counts
    matched = segment_ids[:, None] == jnp.arange(slot_count, dtype=jnp.int32)[None, :]
    start_tok = jnp.sum(jnp.where(matched, starts[None, :], 0), axis=1)
    side_tok = jnp.sum(jnp.where(matched, image_sides[None, :], 0), axis=1)
    live_slot = segment_ids < slot_count
    slot_index = jnp.arange(segment_ids.shape[0], dtype=jnp.int32)
    patch_index = jnp.where(live_slot, slot_index - start_tok, 0)
    side_tok = jnp.where(live_slot, side_tok, 1)
    row_index = patch_index // side_tok
    col_index = patch_index - row_index * side_tok
    return (col_index.astype(jnp.float32), row_index.astype(jnp.float32))


def rotate_pairs(rotate_in, freq_table, col_pos, row_pos):
    half_size = rotate_in.shape[-1] // 2
    angles = (
        col_pos[:, None, None] * freq_table[None, :, 0, :]
        + row_pos[:, None, None] * freq_table[None, :, 1, :]
    )
    cosine = jnp.cos(angles)[:, None]
    sine_part = jnp.sin(angles)[:, None]
    first_half = rotate_in[..., :half_size]
    second_half = rotate_in[..., half_size:]
    return jnp.concatenate(
        [
            first_half * cosine - second_half * sine_part,
            first_half * sine_part + second_half * cosine,
        ],
        axis=-1,
    )


def attend_forward(queries, keys, values_v, segment_ids, block_rows):
    row_total, head_count, head_size = queries.shape
    score_scale = head_size ** (-0.5)

    def one_block(pieces):
        query_blk, segment_blk = pieces
        scores = (
            jnp.einsum("qhd,khd->hqk", query_blk, keys, preferred_element_type=jnp.float32)
            * score_scale
        )
        allowed = segment_blk[:, None] == segment_ids[None, :]
        scores = jnp.where(allowed[None], scores, -1e30)
        row_top = jnp.max(scores, axis=-1, keepdims=True)
        exponent = jnp.exp(scores - row_top)
        row_sum = jnp.sum(exponent, axis=-1, keepdims=True)
        soft_weights = (exponent / row_sum).astype(jnp.bfloat16)
        mixed = jnp.einsum(
            "hqk,khd->qhd", soft_weights, values_v, preferred_element_type=jnp.float32
        )
        return (mixed.astype(jnp.bfloat16), (row_top + jnp.log(row_sum))[..., 0])

    blocks = (
        queries.reshape(row_total // block_rows, block_rows, head_count, head_size),
        segment_ids.reshape(row_total // block_rows, block_rows),
    )
    mixed_heads, log_totals = lax.map(one_block, blocks)
    return (mixed_heads.reshape(row_total, head_count * head_size), log_totals)


def attend_backward(queries, keys, values_v, grad_heads, log_totals, segment_ids, block_rows):
    row_total, head_count, head_size = queries.shape
    score_scale = head_size ** (-0.5)

    def one_block(carried, pieces):
        grad_keys, grad_values = carried
        query_blk, grad_blk, total_blk, segment_blk = pieces
        scores = (
            jnp.einsum("qhd,khd->hqk", query_blk, keys, preferred_element_type=jnp.float32)
            * score_scale
        )
        allowed = segment_blk[:, None] == segment_ids[None, :]
        soft_weights = jnp.where(allowed[None], jnp.exp(scores - total_blk[..., None]), 0.0)
        low_weights = soft_weights.astype(jnp.bfloat16)
        grad_weights = jnp.einsum(
            "qhd,khd->hqk", grad_blk, values_v, preferred_element_type=jnp.float32
        )
        inner_sum = jnp.sum(grad_weights * soft_weights, axis=-1, keepdims=True)
        grad_scores = (soft_weights * (grad_weights - inner_sum)).astype(jnp.bfloat16)
        grad_query = (
            jnp.einsum("hqk,khd->qhd", grad_scores, keys, preferred_element_type=jnp.float32)
            * score_scale
        )
        grad_keys = (
            grad_keys
            + jnp.einsum("hqk,qhd->khd", grad_scores, query_blk, preferred_element_type=jnp.float32)
            * score_scale
        )
        grad_values = grad_values + jnp.einsum(
            "hqk,qhd->khd", low_weights, grad_blk, preferred_element_type=jnp.float32
        )
        return ((grad_keys, grad_values), grad_query)

    block_count = row_total // block_rows
    zero_init = jnp.zeros((row_total, head_count, head_size), jnp.float32)
    pieces = (
        queries.reshape(block_count, block_rows, head_count, head_size),
        grad_heads.reshape(block_count, block_rows, head_count, head_size),
        log_totals,
        segment_ids.reshape(block_count, block_rows),
    )
    (grad_keys, grad_values), grad_queries = lax.scan(one_block, (zero_init, zero_init), pieces)
    return (grad_queries.reshape(row_total, head_count, head_size), grad_keys, grad_values)


def on_device(
    tokens,
    cotangent,
    counts,
    sides,
    segments,
    norm1_gain,
    norm1_shift,
    w_qkv,
    b_qkv,
    freqs,
    w_out,
    b_out,
    norm2_gain,
    norm2_shift,
    w_fc1,
    b_fc1,
    w_fc2,
    b_fc2,
):
    row_total = tokens.shape[0]
    pack_count = counts.shape[0]
    pack_rows = row_total // pack_count
    head_count = freqs.shape[0]
    local_width = w_qkv.shape[2]
    head_size = local_width // head_count
    block_rows = min(512, pack_rows)
    segment_packs = segments.reshape(pack_count, pack_rows)
    col_packs, row_packs = jax.vmap(positions)(segment_packs, counts, sides)
    col_pos = col_packs.reshape(row_total)
    row_pos = row_packs.reshape(row_total)
    residual = tokens.astype(jnp.float32)
    normed_one, scaled_one, inverse_one = layer_stats(residual, norm1_gain, norm1_shift)
    low_normed_one = normed_one.astype(jnp.bfloat16)
    projected = (
        jnp.einsum("td,dcj->tcj", low_normed_one, w_qkv, preferred_element_type=jnp.float32)
        + b_qkv[None]
    )
    rotate_in = projected[:, :2].reshape(row_total, 2, head_count, head_size)

    def turn(pairs_in, freq_table):
        return rotate_pairs(pairs_in, freq_table, col_pos, row_pos)

    turned = turn(rotate_in, freqs)
    queries = turned[:, 0].astype(jnp.bfloat16)
    keys = turned[:, 1].astype(jnp.bfloat16)
    values_v = projected[:, 2].reshape(row_total, head_count, head_size).astype(jnp.bfloat16)
    pack_shape = (pack_count, pack_rows, head_count, head_size)
    query_packs = queries.reshape(pack_shape)
    key_packs = keys.reshape(pack_shape)
    value_packs = values_v.reshape(pack_shape)

    def forward_pack(pieces):
        return attend_forward(pieces[0], pieces[1], pieces[2], pieces[3], block_rows)

    mixed_packs, log_totals = lax.map(
        forward_pack, (query_packs, key_packs, value_packs, segment_packs)
    )
    mixed_heads = mixed_packs.reshape(row_total, local_width)
    partial_attn = jnp.dot(mixed_heads, w_out, preferred_element_type=jnp.float32)
    middle = residual + lax.psum(partial_attn, "tensor") + b_out
    normed_two, scaled_two, inverse_two = layer_stats(middle, norm2_gain, norm2_shift)
    low_normed_two = normed_two.astype(jnp.bfloat16)
    hidden_pre = jnp.dot(low_normed_two, w_fc1, preferred_element_type=jnp.float32) + b_fc1
    hidden = jax.nn.gelu(hidden_pre, approximate=False).astype(jnp.bfloat16)
    partial_mlp = jnp.dot(hidden, w_fc2, preferred_element_type=jnp.float32)
    block_output = (
        middle + lax.psum(partial_mlp.astype(jnp.bfloat16), "tensor").astype(jnp.float32) + b_fc2
    ).astype(jnp.bfloat16)
    grad_output = cotangent.astype(jnp.float32)
    grad_fc2_bias = jnp.sum(grad_output, axis=0)
    grad_fc2 = jnp.einsum("tf,td->fd", hidden, cotangent, preferred_element_type=jnp.float32)
    grad_hidden = jnp.einsum("td,fd->tf", cotangent, w_fc2, preferred_element_type=jnp.float32)
    unused, gelu_pull = jax.vjp(
        lambda pre_values: jax.nn.gelu(pre_values, approximate=False), hidden_pre
    )
    grad_pre = gelu_pull(grad_hidden)[0].astype(jnp.bfloat16)
    grad_fc1_bias = jnp.sum(grad_pre.astype(jnp.float32), axis=0)
    grad_fc1 = jnp.einsum("td,tf->df", low_normed_two, grad_pre, preferred_element_type=jnp.float32)
    partial_norm_two = jnp.einsum("tf,df->td", grad_pre, w_fc1, preferred_element_type=jnp.float32)
    grad_normed_two = lax.psum(partial_norm_two, "tensor")
    grad_middle = grad_output + norm_back(grad_normed_two, scaled_two, inverse_two, norm2_gain)
    low_grad_middle = grad_middle.astype(jnp.bfloat16)
    grad_gain_two = jnp.sum(grad_normed_two * scaled_two, axis=0)
    grad_shift_two = jnp.sum(grad_normed_two, axis=0)
    grad_out_bias = jnp.sum(low_grad_middle.astype(jnp.float32), axis=0)
    grad_out_weight = jnp.einsum(
        "tj,td->jd", mixed_heads, low_grad_middle, preferred_element_type=jnp.float32
    )
    grad_mixed = jnp.einsum("td,jd->tj", low_grad_middle, w_out, preferred_element_type=jnp.float32)
    grad_mixed = grad_mixed.astype(jnp.bfloat16).reshape(pack_shape)

    def backward_pack(pieces):
        return attend_backward(
            pieces[0], pieces[1], pieces[2], pieces[3], pieces[4], pieces[5], block_rows
        )

    grad_query_packs, grad_key_packs, grad_value_packs = lax.map(
        backward_pack, (query_packs, key_packs, value_packs, grad_mixed, log_totals, segment_packs)
    )
    grad_queries = grad_query_packs.reshape(row_total, head_count, head_size)
    grad_keys = grad_key_packs.reshape(row_total, head_count, head_size)
    grad_values = grad_value_packs.reshape(row_total, head_count, head_size)
    unused, rotate_pull = jax.vjp(turn, rotate_in, freqs)
    grad_rotate_in, grad_freqs = rotate_pull(jnp.stack([grad_queries, grad_keys], axis=1))
    grad_projected = jnp.concatenate(
        [
            grad_rotate_in.reshape(row_total, 2, local_width),
            grad_values.reshape(row_total, 1, local_width),
        ],
        axis=1,
    ).astype(jnp.bfloat16)
    grad_qkv_bias = jnp.sum(grad_projected.astype(jnp.float32), axis=0)
    grad_qkv = jnp.einsum(
        "td,tcj->dcj", low_normed_one, grad_projected, preferred_element_type=jnp.float32
    )
    partial_norm_one = jnp.einsum(
        "tcj,dcj->td", grad_projected, w_qkv, preferred_element_type=jnp.float32
    )
    grad_normed_one = lax.psum(partial_norm_one.astype(jnp.bfloat16), "tensor").astype(jnp.float32)
    token_grad = grad_middle + norm_back(grad_normed_one, scaled_one, inverse_one, norm1_gain)
    grad_gain_one = jnp.sum(grad_normed_one * scaled_one, axis=0)
    grad_shift_one = jnp.sum(grad_normed_one, axis=0)
    summed = lax.psum(
        (
            grad_gain_one,
            grad_shift_one,
            grad_qkv,
            grad_qkv_bias,
            grad_freqs,
            grad_out_weight,
            grad_out_bias,
            grad_gain_two,
            grad_shift_two,
            grad_fc1,
            grad_fc1_bias,
            grad_fc2,
            grad_fc2_bias,
        ),
        "dp",
    )
    return (
        block_output,
        token_grad,
        summed[0],
        summed[1],
        summed[2],
        summed[3],
        summed[4],
        summed[5],
        summed[6],
        summed[7],
        summed[8],
        summed[9],
        summed[10],
        summed[11],
        summed[12],
    )


def solution(mesh):
    in_specs = (
        P("dp", None),
        P("dp", None),
        P("dp", None),
        P("dp", None),
        P("dp"),
        P(),
        P(),
        P(None, None, "tensor"),
        P(None, "tensor"),
        P("tensor", None, None),
        P("tensor", None),
        P(),
        P(),
        P(),
        P(None, "tensor"),
        P("tensor"),
        P("tensor", None),
        P(),
    )
    out_specs = (
        P("dp", None),
        P("dp", None),
        P(),
        P(),
        P(None, None, "tensor"),
        P(None, "tensor"),
        P("tensor", None, None),
        P("tensor", None),
        P(),
        P(),
        P(),
        P(None, "tensor"),
        P("tensor"),
        P("tensor", None),
        P(),
    )
    return jax.shard_map(
        on_device, mesh=mesh, in_specs=in_specs, out_specs=out_specs, check_vma=False
    )
```

profile of v0, /device:TPU:0, one launch (start us, length us, event | category | flops | bytes accessed | tf_op | source)
XLA Modules:
  0.0 858.8 jit_solution(9181087721669908261)
XLA Ops:
  7.3 2.5 convert_reduce_fusion.1
  9.9 2.9 fusion.54
  12.9 2.3 fusion.74
  15.8 1.9 slice.39
  20.1 2.8 fusion.66
  23.0 3.0 multiply_subtract_fusion
  29.6 33.4 %while.54 = (s32[]{:T(128)}, bf16[2,1024,192]{1,2,0:T(8,128)(2,1)}, f32[2,2,3,512]{3,2,1,0:T(4,128)}, bf16[2,1024,3,64]{1,3,2,0:T(8,128)(2,1)}, s32[2,1024]{1,0:...) while((s32[]{:T(128)}, bf16[2,1024,192]{1,2,0:T(8,128)(2,1)}, ...), condition=%wide.region_10.11_spmd, body=%wide.region_5.10_spmd.sunk | while | flops 422148608 | bytes 28762504 | solution.py:186
  33.6 11.3 %while.57 = (s32[]{:T(128)}, bf16[2,512,3,64]{1,3,2,0:T(8,128)(2,1)S(1)}, f32[2,3,512]{2,1,0:T(4,128)S(1)}, s32[2,512]{1,0:T(2,128)S(1)}, s32[1024]{0:T(1024)S(1...) while((s32[]{:T(128)}, ...), condition=%wide.region_9.9_spmd, body=%wide.region_6.8_spmd.sunk | while | flops 422148608 | bytes 22220916 | solution.py:82
  35.4 1.8 fusion.153
  37.2 2.1 fusion.154
  41.1 1.8 fusion.153
  42.8 2.1 fusion.154
  50.2 11.3 %while.57 = (s32[]{:T(128)}, bf16[2,512,3,64]{1,3,2,0:T(8,128)(2,1)S(1)}, f32[2,3,512]{2,1,0:T(4,128)S(1)}, s32[2,512]{1,0:T(2,128)S(1)}, s32[1024]{0:T(1024)S(1...) while((s32[]{:T(128)}, ...), condition=%wide.region_9.9_spmd, body=%wide.region_6.8_spmd.sunk | while | flops 422148608 | bytes 22220916 | solution.py:82
  52.0 1.8 fusion.153
  53.8 2.1 fusion.154
  57.7 1.8 fusion.153
  59.4 2.1 fusion.154
  65.2 3.7 fusion.84
  69.0 122.4 %all-reduce.12.cloned.1.call-done = f32[2048,768]{1,0:T(8,128)} async-done(((f32[2048,768]{1,0:T(8,128)}), f32[2048,768]{1,0:T(8,128)}) %all-reduce.12.cloned.1.call-update) | async-done | bytes 6291472 | tf_op jit(solution)/shard_map/psum | solution.py:191
  191.4 4.6 fusion.80
  199.1 2.6 fusion.85
  202.1 19.1 %convert_reduce_fusion.3 = (f32[768]{0:T(1024)}, bf16[2048,768]{1,0:T(8,128)(2,1)S(1)}, f32[2048,768]{1,0:T(8,128)}) fusion(f32[2048,768]{1,0:T(8,128)S(1)} %fusion.85, f32[768]{0:T(1024)S(1)} %copy-done.54, bf16[2048,768]{1,0:T(8,128)(2,1)S(1)} %copy-done.22, bf16[768,768]{1,0:T(8,128)(2,1)S(1)} %copy-done), kind=kOutput, calls=%fused_computation.92 | convolution fusion | flops 2533883136 | bytes 20060160 | tf_op jit(solution)/shard_map/td,fd->tf/dot_general | solution.py:203
  222.8 4.5 fusion.86
  227.4 5.5 multiply_convert_fusion.1
  234.6 4.0 convolution_convert_fusion
  238.5 108.8 %all-reduce.14.cloned.1.call-done = f32[2048,768]{1,0:T(8,128)} async-done(((f32[2048,768]{1,0:T(8,128)}), f32[2048,768]{1,0:T(8,128)}) %all-reduce.14.cloned.1.call-update) | async-done | bytes 6291472 | tf_op jit(solution)/shard_map/psum | solution.py:211
  347.3 6.6 multiply_reduce_fusion.1
  354.7 5.8 convert_reduce_fusion.4
  360.5 2.6 copy-done.3
  366.0 99.6 %while.56 = (s32[]{:T(128)}, f32[2,1024,3,64]{3,2,1,0:T(4,128)}, f32[2,1024,3,64]{1,0,3,2:T(2,128)}, bf16[2,1024,3,64]{1,3,2,0:T(8,128)(2,1)}, bf16[2,1024,3,64]...) while((s32[]{:T(128)}, f32[2,1024,3,64]{3,2,1,0:T(4,128)}, ...), condition=%wide.region_22.23_spmd, body=%wide.region_18.22_spmd.sunk | while | flops 1031830016 | bytes 76714544 | solution.py:228
  372.3 24.1 %while.58 = (s32[]{:T(128)}, f32[1024,3,64]{0,2,1:T(8,128)S(1)}, f32[1024,3,64]{0,2,1:T(8,128)S(1)}, f32[2,512,3,64]{1,3,2,0:T(8,128)}, bf16[2,512,3,64]{1,3,2,0...) while((s32[]{:T(128)}, f32[1024,3,64]{0,2,1:T(8,128)S(1)}, ...), condition=%wide.region_21.21_spmd.clone, body=%wide.region_19.20_spmd.clone.sunk | while | flops 1031830016 | bytes 61137120 | solution.py:127
  375.0 1.7 fusion.148
  376.7 2.6 multiply_reduce_fusion.12
  379.3 1.9 multiply_convert_fusion.3
  388.8 2.6 multiply_reduce_fusion.12
  391.4 1.9 multiply_convert_fusion.3
  397.1 14.4 %dynamic_update_slice.50 = f32[2,1024,3,64]{1,0,3,2:T(2,128)} dynamic-update-slice(f32[2,1024,3,64]{1,0,3,2:T(2,128)} %get-tuple-element.988, f32[1,1024,3,64]{1,0,3,2:T(1,128)S(1)} %copy.167, s32[]{:T(128)S(6)} %copy.212, s32[]{:T(128)} %constant.61.clone.1..sunk.1, s32[]{:T(128)} %constant.61.clone.1..sunk.1, s32[]{:T(128)} %constant.61.clone.1..sunk.1) | dynamic-update-slice | bytes 1572868 | tf_op jit(solution)/shard_map/while/body/jit(dynamic_update_index_in_dim)/dynamic_update_slice | solution.py:228
  412.3 1.8 copy.166
  414.1 1.7 bitcast_dynamic-update-slice_fusion.9
  422.0 24.1 %while.58 = (s32[]{:T(128)}, f32[1024,3,64]{0,2,1:T(8,128)S(1)}, f32[1024,3,64]{0,2,1:T(8,128)S(1)}, f32[2,512,3,64]{1,3,2,0:T(8,128)}, bf16[2,512,3,64]{1,3,2,0...) while((s32[]{:T(128)}, f32[1024,3,64]{0,2,1:T(8,128)S(1)}, ...), condition=%wide.region_21.21_spmd.clone, body=%wide.region_19.20_spmd.clone.sunk | while | flops 1031830016 | bytes 61137120 | solution.py:127
  426.5 2.6 multiply_reduce_fusion.12
  429.1 1.9 multiply_convert_fusion.3
  438.5 2.6 multiply_reduce_fusion.12
  441.1 1.9 multiply_convert_fusion.3
  446.9 14.4 %dynamic_update_slice.50 = f32[2,1024,3,64]{1,0,3,2:T(2,128)} dynamic-update-slice(f32[2,1024,3,64]{1,0,3,2:T(2,128)} %get-tuple-element.988, f32[1,1024,3,64]{1,0,3,2:T(1,128)S(1)} %copy.167, s32[]{:T(128)S(6)} %copy.212, s32[]{:T(128)} %constant.61.clone.1..sunk.1, s32[]{:T(128)} %constant.61.clone.1..sunk.1, s32[]{:T(128)} %constant.61.clone.1..sunk.1) | dynamic-update-slice | bytes 1572868 | tf_op jit(solution)/shard_map/while/body/jit(dynamic_update_index_in_dim)/dynamic_update_slice | solution.py:228
  462.1 1.8 copy.166
  463.9 1.7 bitcast_dynamic-update-slice_fusion.9
  465.6 1.9 copy.100
  468.1 3.4 copy.102
  471.5 3.6 stack_reshape.7
  475.1 5.4 multiply_reduce_fusion.7
  481.7 4.0 bitcast_convert_fusion
  485.8 7.1 fusion.87
  492.9 4.2 fusion.88
  499.0 3.6 fusion.72
  503.7 4.7 multiply_reduce_fusion.10
  508.8 96.9 %all-reduce.18.cloned.1.call-done = (bf16[2048,768]{1,0:T(8,128)(2,1)}, bf16[2048,768]{1,0:T(8,128)(2,1)}) async-done(((bf16[2048,768]{1,0:T(8,128)(2,1)}, bf16[2048,768]{1,0:T(8,128)(2,1)}), (bf16[2048,768]{1,0:T(8,128)(2,1)}, bf16[2048,768]{1,0:T(8,128)(2,1)})) %all-reduce.18.cloned.1.call-update) | async-done | bytes 6291472 | tf_op jit(solution)/shard_map/psum | solution.py:198
  605.7 5.2 fusion.58
  611.0 41.4 %all-reduce.4 = (f32[768]{0:T(1024)}, f32[768]{0:T(1024)}, f32[3,192]{1,0:T(4,128)}, f32[3,2,32]{2,0,1:T(4,128)S(1)}, f32[768]{0:T(1024)}, /*index=5*/f32[768]{0...) all-reduce(f32[768]{0:T(1024)S(1)} %get-tuple-element.437, ...), channel_id=1, replica_groups=mesh['dp'=8,'tensor'=4] {'dp'}, use_global_device_ids=true, to_apply=%region_27.28 | all-reduce | flops 6144 | bytes 49152 | tf_op jit(solution)/shard_map/psum | solution.py:254
  653.0 6.6 add_convert_fusion.1
  661.6 4.2 fusion.53
  665.9 178.3 %all-reduce.16.cloned.1.call-done = (f32[768,3,192]{0,2,1:T(8,128)}, f32[192,768]{1,0:T(8,128)}, f32[768,768]{1,0:T(8,128)}, f32[768,768]{1,0:T(8,128)}) async-done(((f32[768,3,192]{0,2,1:T(8,128)}, f32[192,768]{1,0:T(8,128)}, f32[768,768]{1,0:T(8,128)}, f32[768,768]{1,0:T(8,128)}), (f32[768,3,192]{0,2,1:T(8,128)}, f32[192,768]{1,0:T(8,128)}, f32[768,768]{1,0:T(8,128)}, ...) | async-done | bytes 7077904 | tf_op jit(solution)/shard_map/psum | solution.py:254
  844.2 2.9 copy.228
  847.1 1.9 copy.229
  (320 shorter events, 91.0 us)
Async XLA Ops:
  7.2 194.5 %copy-start = (bf16[768,768]{1,0:T(8,128)(2,1)S(1)}, bf16[768,768]{1,0:T(8,128)(2,1)}, u32[]{:S(2)}) copy-start(bf16[768,768]{1,0:T(8,128)(2,1)} %param.42) | copy-start | bytes 3538948
  7.2 5.6 copy-start.50
  7.2 5.6 copy-start.64
  7.2 5.6 copy-start.62
  7.2 184.2 %all-reduce.12.cloned.1.call-start = ((), (), s32[]{:S(2)}) async-start(), calls=%async_computation | async-start | bytes 12582912 | tf_op jit(solution)/shard_map/psum | solution.py:191
  7.3 5.6 copy-start.4
  9.8 5.4 copy-start.32
  12.8 2.4 copy-start.36
  12.9 2.3 copy-start.52
  15.6 2.0 copy-start.57
  15.6 2.3 copy-start.59
  15.6 2.3 copy-start.60
  15.6 2.4 copy-start.41
  18.3 7.7 copy-start.34
  18.4 7.6 copy-start.38
  20.1 5.9 copy-start.42
  20.1 5.9 copy-start.44
  23.0 3.3 copy-start.13
  23.0 3.3 copy-start.15
  29.6 35.5 %copy-start.27 = (bf16[192,768]{1,0:T(8,128)(2,1)S(1)}, bf16[192,768]{1,0:T(8,128)(2,1)}, u32[]{:S(2)}) copy-start(bf16[192,768]{1,0:T(8,128)(2,1)} %param.36) | copy-start | bytes 884740
  33.6 11.4 %copy-start.30 = (f32[2,2,3,512]{3,2,1,0:T(4,128)S(1)}, f32[2,2,3,512]{3,2,1,0:T(4,128)}, u32[]{:S(2)}) copy-start(f32[2,2,3,512]{3,2,1,0:T(4,128)} %get-tuple-element.954) | copy-start | bytes 73732 | tf_op jit(solution)/shard_map/while
  50.2 11.4 %copy-start.30 = (f32[2,2,3,512]{3,2,1,0:T(4,128)S(1)}, f32[2,2,3,512]{3,2,1,0:T(4,128)}, u32[]{:S(2)}) copy-start(f32[2,2,3,512]{3,2,1,0:T(4,128)} %get-tuple-element.954) | copy-start | bytes 73732 | tf_op jit(solution)/shard_map/while
  65.2 126.2 %copy-start.58 = (f32[768]{0:T(1024)S(1)}, f32[768]{0:T(1024)}, u32[]{:S(2)}) copy-start(f32[768]{0:T(1024)} %param.37) | copy-start | bytes 9220
  68.9 278.4 %all-reduce.14.cloned.1.call-start = ((), (), s32[]{:S(2)}) async-start(), calls=%async_computation.1 | async-start | bytes 12582912 | tf_op jit(solution)/shard_map/psum | solution.py:211
  196.0 2.7 copy-start.2
  196.9 2.2 copy-start.61
  199.1 2.6 copy-start.19
  199.1 3.0 copy-start.22
  199.1 3.0 copy-start.54
  202.1 19.1 %copy-start.17 = (f32[2048,768]{1,0:T(8,128)}, f32[2048,768]{1,0:T(8,128)S(1)}, u32[]{:S(2)}) copy-start(f32[2048,768]{1,0:T(8,128)S(1)} %fusion.85) | copy-start | bytes 18874372
  227.4 378.4 %all-reduce.18.cloned.1.call-start = ((), (), s32[]{:S(2)}) async-start(), calls=%async_computation.3 | async-start | bytes 12582912 | tf_op jit(solution)/shard_map/psum | solution.py:198
  347.3 6.7 copy-start.7
  347.3 7.4 copy-start.23
  360.5 2.6 copy-start.3
  366.1 2.4 copy-start.28
  396.3 19.5 %copy-start.29 = (s32[2,1024]{1,0:T(2,128)S(1)}, s32[2,1024]{1,0:T(2,128)}, u32[]{:S(2)}) copy-start(s32[2,1024]{1,0:T(2,128)} %copy-done.28) | copy-start | bytes 24580 | tf_op jit(solution)/shard_map/while
  415.9 2.4 copy-start.28
  446.1 19.5 %copy-start.29 = (s32[2,1024]{1,0:T(2,128)S(1)}, s32[2,1024]{1,0:T(2,128)}, u32[]{:S(2)}) copy-start(s32[2,1024]{1,0:T(2,128)} %copy-done.28) | copy-start | bytes 24580 | tf_op jit(solution)/shard_map/while
  475.1 5.4 copy-start.14
  475.1 5.4 copy-start.16
  485.7 358.4 %all-reduce.16.cloned.1.call-start = ((), (), s32[]{:S(2)}) async-start(), calls=%async_computation.2 | async-start | bytes 14155776 | tf_op jit(solution)/shard_map/psum | solution.py:254
  485.8 7.1 copy-start.21
  485.8 7.1 copy-start.24
  485.8 11.5 %slice-start = ((s8[6291456]{0:T(1024)(128)(4,1)}), s8[4194304]{0:T(1024)(128)(4,1)S(1)}, s32[]{:S(2)}) async-start(s8[6291456]{0:T(1024)(128)(4,1)} %bitcast.219), calls=%async_computation.4 | async-start | bytes 8388608
  492.9 4.4 slice-start.1
  492.9 4.4 copy-start.12
  497.0 1.9 copy-start.5
  497.0 1.9 copy-start.33
  497.1 1.9 copy-start.37
  497.1 1.9 copy-start.51
  497.1 1.9 copy-start.65
  502.6 108.3 %copy-start.46 = (f32[768]{0:T(1024)S(1)}, f32[768]{0:T(1024)}, u32[]{:S(2)}) copy-start(f32[768]{0:T(1024)} %get-tuple-element.435) | copy-start | bytes 9220
  502.6 108.3 %copy-start.47 = (f32[768]{0:T(1024)S(1)}, f32[768]{0:T(1024)}, u32[]{:S(2)}) copy-start(f32[768]{0:T(1024)} %get-tuple-element.440) | copy-start | bytes 9220
  502.6 108.3 %copy-start.48 = (f32[768]{0:T(1024)S(1)}, f32[768]{0:T(1024)}, u32[]{:S(2)}) copy-start(f32[768]{0:T(1024)} %get-tuple-element.547) | copy-start | bytes 9220
  502.7 108.3 %copy-start.49 = (f32[768]{0:T(1024)S(1)}, f32[768]{0:T(1024)}, u32[]{:S(2)}) copy-start(f32[768]{0:T(1024)} %get-tuple-element.569) | copy-start | bytes 9220
  502.7 108.3 %copy-start.56 = (f32[768]{0:T(1024)S(1)}, f32[768]{0:T(1024)}, u32[]{:S(2)}) copy-start(f32[768]{0:T(1024)} %get-tuple-element.544) | copy-start | bytes 9220
  502.7 150.2 %copy-start.55 = (f32[768]{0:T(1024)S(1)}, f32[768]{0:T(1024)}, u32[]{:S(2)}) copy-start(f32[768]{0:T(1024)} %param.43) | copy-start | bytes 9220
  605.7 53.8 %slice-start.2 = ((s8[6291456]{0:T(1024)(128)(4,1)}), s8[2097152]{0:T(1024)(128)(4,1)S(1)}, s32[]{:S(2)}) async-start(s8[6291456]{0:T(1024)(128)(4,1)} %bitcast.221), calls=%async_computation.6 | async-start | bytes 4194304
  652.9 6.6 slice-start.3
  652.9 7.4 copy-start.6
  652.9 8.7 %copy-start.10 = (bf16[2048,768]{1,0:T(8,128)(2,1)S(1)}, bf16[2048,768]{1,0:T(8,128)(2,1)}, u32[]{:S(2)}) copy-start(bf16[2048,768]{1,0:T(8,128)(2,1)} %get-tuple-element.539) | copy-start | bytes 9437188
  844.2 4.9 copy-start.26
  844.2 6.3 copy-start.25
  844.2 7.7 copy-start.1
  (21 other events, 23.9 us)
Sparse Core Ops, SparseCore 0:
  69.1 122.2 all-reduce.11
  227.5 119.7 all-reduce.13
  485.9 119.8 all-reduce.17
  611.1 232.9 all-reduce.15
where the time goes:
time: 870 us; the launch traced here: 859 us
  waiting for transfers between devices  506 us (58%)
  local copies, waits for them, and re-layouts  110 us (13%)
  matrix products  100 us (11%)
  other arithmetic  84.9 us (10%)
  blocking collectives  41.4 us (5%)
  between operations  15 us (2%)
    psum x1, waiting for transfers between devices, on_device(): lax.psum((grad_gain_one, grad_shift_one, grad_qkv, grad_qkv_bias, grad_fr...  178 us
    psum x1, waiting for transfers between devices, on_device(): middle = residual + lax.psum(partial_attn, 'tensor') + b_out  122 us
    psum x1, waiting for transfers between devices, on_device(): grad_normed_two = lax.psum(partial_norm_two, 'tensor')  109 us
    psum x1, waiting for transfers between devices, on_device(): lax.psum(partial_mlp.astype(jnp.bfloat16), 'tensor').astype(jnp.float32)  96.9 us
    psum x1, blocking collectives, on_device(): lax.psum((grad_gain_one, grad_shift_one, grad_qkv, grad_qkv_bias, grad_fr...  41.4 us
    dynamic_update_slice x8, local copies, waits for them, and re-layouts, on_device(): lax.map(backward_pack, (query_packs, key_packs, value_packs, grad_mixed,...  35.4 us
    unnamed x137, local copies, waits for them, and re-layouts  20.6 us
    dot_general x1, matrix products, on_device(): jnp.einsum('td,fd->tf', cotangent, w_fc2, preferred_element_type=jnp.floa...  19.1 us
  transfers between devices with their start and end apart: 4, of which 4 were waited for; matrix products, arithmetic and copies ran while one was open for 6% of the time, Pallas kernels for 0%

commit v1 on v0

--- a/solution.py
+++ b/solution.py
@@ -188,7 +188,7 @@
     )
     mixed_heads = mixed_packs.reshape(row_total, local_width)
     partial_attn = jnp.dot(mixed_heads, w_out, preferred_element_type=jnp.float32)
-    middle = residual + lax.psum(partial_attn, "tensor") + b_out
+    middle = residual + jnp.sum(lax.all_gather(partial_attn, "tensor"), axis=0) + b_out
     normed_two, scaled_two, inverse_two = layer_stats(middle, norm2_gain, norm2_shift)
     low_normed_two = normed_two.astype(jnp.bfloat16)
     hidden_pre = jnp.dot(low_normed_two, w_fc1, preferred_element_type=jnp.float32) + b_fc1

time: 870 us -> 926 us (1.064)
  waiting for transfers between devices: 506 us -> 541 us
  other arithmetic: 84.9 us -> 97.2 us
    all_gather x0 -> x1, waiting for transfers between devices: none -> 158 us  [on_device(): lax.all_gather(partial_attn, 'tensor')]
    psum x1 -> x0, waiting for transfers between devices: 122 us -> none  [on_device(): middle = residual + lax.psum(partial_attn, 'tensor') + b_out]
    reduce_sum x0 -> x1, other arithmetic: none -> 12.7 us  [on_device(): jnp.sum(lax.all_gather(partial_attn, 'tensor'), axis=0)]
  transfers between devices with their start and end apart: 4 -> 4, of which waited for: 4 -> 4; matrix products, arithmetic and copies ran while one was open for 6% -> 5% of each run, Pallas kernels for 0% -> 0%
where the time goes in v1:
time: 926 us; the launch traced here: 915 us
  waiting for transfers between devices  541 us (58%)
  local copies, waits for them, and re-layouts  110 us (12%)
  matrix products  100 us (11%)
  other arithmetic  97.2 us (10%)
  blocking collectives  41.4 us (4%)
  between operations  15 us (2%)
    psum x1, waiting for transfers between devices, on_device(): lax.psum((grad_gain_one, grad_shift_one, grad_qkv, grad_qkv_bias, grad_fr...  178 us
    all_gather x1, waiting for transfers between devices, on_device(): lax.all_gather(partial_attn, 'tensor')  158 us
    psum x1, waiting for transfers between devices, on_device(): grad_normed_two = lax.psum(partial_norm_two, 'tensor')  109 us
    psum x1, waiting for transfers between devices, on_device(): lax.psum(partial_mlp.astype(jnp.bfloat16), 'tensor').astype(jnp.float32)  96.9 us
    psum x1, blocking collectives, on_device(): lax.psum((grad_gain_one, grad_shift_one, grad_qkv, grad_qkv_bias, grad_fr...  41.4 us
    dynamic_update_slice x8, local copies, waits for them, and re-layouts, on_device(): lax.map(backward_pack, (query_packs, key_packs, value_packs, grad_mixed,...  35.4 us
    unnamed x137, local copies, waits for them, and re-layouts  21 us
    dot_general x1, matrix products, on_device(): jnp.einsum('td,fd->tf', cotangent, w_fc2, preferred_element_type=jnp.floa...  19.1 us
  transfers between devices with their start and end apart: 4, of which 4 were waited for; matrix products, arithmetic and copies ran while one was open for 5% of the time, Pallas kernels for 0%

profile of v1, /device:TPU:0, one launch (start us, length us, event | category | flops | bytes accessed | tf_op | source)
XLA Modules:
  0.0 914.6 jit_solution(10092107732566013165)
XLA Ops:
  7.3 2.5 convert_reduce_fusion.1
  9.9 2.9 fusion.54
  12.9 2.3 fusion.74
  15.8 1.9 slice.39
  20.1 2.8 fusion.66
  23.0 3.0 multiply_subtract_fusion
  29.6 33.5 %while.54 = (s32[]{:T(128)}, bf16[2,1024,192]{1,2,0:T(8,128)(2,1)}, f32[2,2,3,512]{3,2,1,0:T(4,128)}, bf16[2,1024,3,64]{1,3,2,0:T(8,128)(2,1)}, s32[2,1024]{1,0:...) while((s32[]{:T(128)}, bf16[2,1024,192]{1,2,0:T(8,128)(2,1)}, ...), condition=%wide.region_10.11_spmd, body=%wide.region_5.10_spmd.sunk | while | flops 422148608 | bytes 28762504 | solution.py:186
  33.7 11.3 %while.57 = (s32[]{:T(128)}, bf16[2,512,3,64]{1,3,2,0:T(8,128)(2,1)S(1)}, f32[2,3,512]{2,1,0:T(4,128)S(1)}, s32[2,512]{1,0:T(2,128)S(1)}, s32[1024]{0:T(1024)S(1...) while((s32[]{:T(128)}, ...), condition=%wide.region_9.9_spmd, body=%wide.region_6.8_spmd.sunk | while | flops 422148608 | bytes 22220916 | solution.py:82
  35.4 1.8 fusion.153
  37.2 2.1 fusion.154
  41.1 1.8 fusion.153
  42.9 2.1 fusion.154
  50.3 11.3 %while.57 = (s32[]{:T(128)}, bf16[2,512,3,64]{1,3,2,0:T(8,128)(2,1)S(1)}, f32[2,3,512]{2,1,0:T(4,128)S(1)}, s32[2,512]{1,0:T(2,128)S(1)}, s32[1024]{0:T(1024)S(1...) while((s32[]{:T(128)}, ...), condition=%wide.region_9.9_spmd, body=%wide.region_6.8_spmd.sunk | while | flops 422148608 | bytes 22220916 | solution.py:82
  52.1 1.8 fusion.153
  53.8 2.1 fusion.154
  57.7 1.8 fusion.153
  59.5 2.1 fusion.154
  65.2 3.7 fusion.84
  69.0 157.6 %all-gather.3.cloned.1.call-done = f32[8192,768]{1,0:T(8,128)} async-done(((f32[2048,768]{1,0:T(8,128)}), f32[8192,768]{1,0:T(8,128)}) %all-gather.3.cloned.1.call-update) | async-done | bytes 25165840 | tf_op jit(solution)/shard_map/all_gather | solution.py:191
  226.6 12.7 %reduce_sum.266 = f32[2048,768]{1,0:T(8,128)} reduce(f32[4,2048,768]{2,1,0:T(8,128)} %bitcast.226, f32[]{:T(128)} %constant.82.clone.1), dimensions={0}, to_apply=%region_11.12 | reduce | flops 4718592 | bytes 31457284 | tf_op jit(solution)/shard_map/reduce_sum | solution.py:191
  239.3 4.6 fusion.80
  247.0 2.6 fusion.85
  250.0 19.1 %convert_reduce_fusion.3 = (f32[768]{0:T(1024)}, bf16[2048,768]{1,0:T(8,128)(2,1)S(1)}, f32[2048,768]{1,0:T(8,128)}) fusion(f32[2048,768]{1,0:T(8,128)S(1)} %fusion.85, f32[768]{0:T(1024)S(1)} %copy-done.54, bf16[2048,768]{1,0:T(8,128)(2,1)S(1)} %copy-done.22, bf16[768,768]{1,0:T(8,128)(2,1)S(1)} %copy-done), kind=kOutput, calls=%fused_computation.92 | convolution fusion | flops 2533883136 | bytes 20060160 | tf_op jit(solution)/shard_map/td,fd->tf/dot_general | solution.py:203
  270.7 4.5 fusion.86
  275.4 5.5 multiply_convert_fusion.1
  282.5 4.0 convolution_convert_fusion
  286.5 108.6 %all-reduce.11.cloned.1.call-done = f32[2048,768]{1,0:T(8,128)} async-done(((f32[2048,768]{1,0:T(8,128)}), f32[2048,768]{1,0:T(8,128)}) %all-reduce.11.cloned.1.call-update) | async-done | bytes 6291472 | tf_op jit(solution)/shard_map/psum | solution.py:211
  395.0 6.6 multiply_reduce_fusion.1
  402.4 5.8 convert_reduce_fusion.4
  408.2 2.6 copy-done.3
  413.7 107.6 %while.56 = (s32[]{:T(128)}, f32[2,1024,3,64]{3,2,1,0:T(4,128)}, f32[2,1024,3,64]{1,0,3,2:T(2,128)}, bf16[2,1024,3,64]{1,3,2,0:T(8,128)(2,1)}, bf16[2,1024,3,64]...) while((s32[]{:T(128)}, f32[2,1024,3,64]{3,2,1,0:T(4,128)}, ...), condition=%wide.region_22.23_spmd, body=%wide.region_18.22_spmd.sunk | while | flops 1031830016 | bytes 76714544 | solution.py:228
  428.0 24.1 %while.58 = (s32[]{:T(128)}, f32[1024,3,64]{0,2,1:T(8,128)S(1)}, f32[1024,3,64]{0,2,1:T(8,128)S(1)}, f32[2,512,3,64]{1,3,2,0:T(8,128)}, bf16[2,512,3,64]{1,3,2,0...) while((s32[]{:T(128)}, f32[1024,3,64]{0,2,1:T(8,128)S(1)}, ...), condition=%wide.region_21.21_spmd.clone, body=%wide.region_19.20_spmd.clone.sunk | while | flops 1031830016 | bytes 61137120 | solution.py:127
  432.5 2.6 multiply_reduce_fusion.12
  435.0 1.9 multiply_convert_fusion.3
  444.5 2.6 multiply_reduce_fusion.12
  447.1 1.9 multiply_convert_fusion.3
  452.9 14.4 %dynamic_update_slice.50 = f32[2,1024,3,64]{1,0,3,2:T(2,128)} dynamic-update-slice(f32[2,1024,3,64]{1,0,3,2:T(2,128)} %get-tuple-element.988, f32[1,1024,3,64]{1,0,3,2:T(1,128)S(1)} %copy.168, s32[]{:T(128)S(6)} %copy.212, s32[]{:T(128)} %constant.61.clone.1..sunk.1, s32[]{:T(128)} %constant.61.clone.1..sunk.1, s32[]{:T(128)} %constant.61.clone.1..sunk.1) | dynamic-update-slice | bytes 1572868 | tf_op jit(solution)/shard_map/while/body/jit(dynamic_update_index_in_dim)/dynamic_update_slice | solution.py:228
  468.0 1.8 copy.167
  469.9 1.7 bitcast_dynamic-update-slice_fusion.9
  477.7 24.1 %while.58 = (s32[]{:T(128)}, f32[1024,3,64]{0,2,1:T(8,128)S(1)}, f32[1024,3,64]{0,2,1:T(8,128)S(1)}, f32[2,512,3,64]{1,3,2,0:T(8,128)}, bf16[2,512,3,64]{1,3,2,0...) while((s32[]{:T(128)}, f32[1024,3,64]{0,2,1:T(8,128)S(1)}, ...), condition=%wide.region_21.21_spmd.clone, body=%wide.region_19.20_spmd.clone.sunk | while | flops 1031830016 | bytes 61137120 | solution.py:127
  482.2 2.6 multiply_reduce_fusion.12
  484.8 1.9 multiply_convert_fusion.3
  494.2 2.6 multiply_reduce_fusion.12
  496.8 1.9 multiply_convert_fusion.3
  502.6 14.4 %dynamic_update_slice.50 = f32[2,1024,3,64]{1,0,3,2:T(2,128)} dynamic-update-slice(f32[2,1024,3,64]{1,0,3,2:T(2,128)} %get-tuple-element.988, f32[1,1024,3,64]{1,0,3,2:T(1,128)S(1)} %copy.168, s32[]{:T(128)S(6)} %copy.212, s32[]{:T(128)} %constant.61.clone.1..sunk.1, s32[]{:T(128)} %constant.61.clone.1..sunk.1, s32[]{:T(128)} %constant.61.clone.1..sunk.1) | dynamic-update-slice | bytes 1572868 | tf_op jit(solution)/shard_map/while/body/jit(dynamic_update_index_in_dim)/dynamic_update_slice | solution.py:228
  517.8 1.8 copy.167
  519.6 1.7 bitcast_dynamic-update-slice_fusion.9
  521.3 1.9 copy.100
  523.8 3.4 copy.102
  527.2 3.6 stack_reshape.7
  530.9 5.4 multiply_reduce_fusion.7
  537.4 4.0 bitcast_convert_fusion
  541.5 7.1 fusion.87
  548.6 4.2 fusion.88
  554.7 3.6 fusion.72
  559.4 4.7 multiply_reduce_fusion.10
  564.5 96.9 %all-reduce.15.cloned.1.call-done = (bf16[2048,768]{1,0:T(8,128)(2,1)}, bf16[2048,768]{1,0:T(8,128)(2,1)}) async-done(((bf16[2048,768]{1,0:T(8,128)(2,1)}, bf16[2048,768]{1,0:T(8,128)(2,1)}), (bf16[2048,768]{1,0:T(8,128)(2,1)}, bf16[2048,768]{1,0:T(8,128)(2,1)})) %all-reduce.15.cloned.1.call-update) | async-done | bytes 6291472 | tf_op jit(solution)/shard_map/psum | solution.py:198
  661.4 5.2 fusion.58
  666.7 41.4 %all-reduce.4 = (f32[768]{0:T(1024)}, f32[768]{0:T(1024)}, f32[3,192]{1,0:T(4,128)}, f32[3,2,32]{2,0,1:T(4,128)S(1)}, f32[768]{0:T(1024)}, /*index=5*/f32[768]{0...) all-reduce(f32[768]{0:T(1024)S(1)} %get-tuple-element.437, ...), channel_id=1, replica_groups=mesh['dp'=8,'tensor'=4] {'dp'}, use_global_device_ids=true, to_apply=%region_27.28 | all-reduce | flops 6144 | bytes 49152 | tf_op jit(solution)/shard_map/psum | solution.py:254
  708.7 6.6 add_convert_fusion.1
  717.4 4.2 fusion.53
  721.6 178.3 %all-reduce.13.cloned.1.call-done = (f32[768,3,192]{0,2,1:T(8,128)}, f32[192,768]{1,0:T(8,128)}, f32[768,768]{1,0:T(8,128)}, f32[768,768]{1,0:T(8,128)}) async-done(((f32[768,3,192]{0,2,1:T(8,128)}, f32[192,768]{1,0:T(8,128)}, f32[768,768]{1,0:T(8,128)}, f32[768,768]{1,0:T(8,128)}), (f32[768,3,192]{0,2,1:T(8,128)}, f32[192,768]{1,0:T(8,128)}, f32[768,768]{1,0:T(8,128)}, ...) | async-done | bytes 7077904 | tf_op jit(solution)/shard_map/psum | solution.py:254
  899.9 2.9 copy.228
  902.9 1.9 copy.229
  (321 shorter events, 92.7 us)
Async XLA Ops:
  7.2 242.5 %copy-start = (bf16[768,768]{1,0:T(8,128)(2,1)S(1)}, bf16[768,768]{1,0:T(8,128)(2,1)}, u32[]{:S(2)}) copy-start(bf16[768,768]{1,0:T(8,128)(2,1)} %param.42) | copy-start | bytes 3538948
  7.2 5.6 copy-start.50
  7.2 5.6 copy-start.64
  7.2 5.6 copy-start.62
  7.2 219.4 %all-gather.3.cloned.1.call-start = ((), (), s32[]{:S(2)}) async-start(), calls=%async_computation.1 | async-start | bytes 31457280 | tf_op jit(solution)/shard_map/all_gather | solution.py:191
  7.3 5.6 copy-start.4
  9.8 5.4 copy-start.32
  12.8 2.4 copy-start.36
  12.9 2.3 copy-start.52
  15.6 2.0 copy-start.57
  15.6 2.3 copy-start.59
  15.6 2.3 copy-start.60
  15.6 2.4 copy-start.41
  18.3 7.7 copy-start.34
  18.4 7.6 copy-start.38
  20.1 5.9 copy-start.42
  20.1 5.9 copy-start.44
  23.0 3.3 copy-start.13
  23.0 3.3 copy-start.15
  29.6 35.6 %copy-start.27 = (bf16[192,768]{1,0:T(8,128)(2,1)S(1)}, bf16[192,768]{1,0:T(8,128)(2,1)}, u32[]{:S(2)}) copy-start(bf16[192,768]{1,0:T(8,128)(2,1)} %param.36) | copy-start | bytes 884740
  33.6 11.4 %copy-start.30 = (f32[2,2,3,512]{3,2,1,0:T(4,128)S(1)}, f32[2,2,3,512]{3,2,1,0:T(4,128)}, u32[]{:S(2)}) copy-start(f32[2,2,3,512]{3,2,1,0:T(4,128)} %get-tuple-element.954) | copy-start | bytes 73732 | tf_op jit(solution)/shard_map/while
  50.3 11.4 %copy-start.30 = (f32[2,2,3,512]{3,2,1,0:T(4,128)S(1)}, f32[2,2,3,512]{3,2,1,0:T(4,128)}, u32[]{:S(2)}) copy-start(f32[2,2,3,512]{3,2,1,0:T(4,128)} %get-tuple-element.954) | copy-start | bytes 73732 | tf_op jit(solution)/shard_map/while
  69.0 326.0 %all-reduce.11.cloned.1.call-start = ((), (), s32[]{:S(2)}) async-start(), calls=%async_computation | async-start | bytes 12582912 | tf_op jit(solution)/shard_map/psum | solution.py:211
  226.6 12.7 %copy-start.58 = (f32[768]{0:T(1024)S(1)}, f32[768]{0:T(1024)}, u32[]{:S(2)}) copy-start(f32[768]{0:T(1024)} %param.37) | copy-start | bytes 9220
  243.9 2.7 copy-start.2
  244.9 2.2 copy-start.61
  247.0 2.6 copy-start.19
  247.0 3.0 copy-start.22
  247.0 3.0 copy-start.54
  250.0 19.1 %copy-start.17 = (f32[2048,768]{1,0:T(8,128)}, f32[2048,768]{1,0:T(8,128)S(1)}, u32[]{:S(2)}) copy-start(f32[2048,768]{1,0:T(8,128)S(1)} %fusion.85) | copy-start | bytes 18874372
  275.3 386.2 %all-reduce.15.cloned.1.call-start = ((), (), s32[]{:S(2)}) async-start(), calls=%async_computation.3 | async-start | bytes 12582912 | tf_op jit(solution)/shard_map/psum | solution.py:198
  395.0 6.7 copy-start.7
  395.0 7.4 copy-start.23
  408.2 2.6 copy-start.3
  421.8 2.4 copy-start.28
  452.0 19.5 %copy-start.29 = (s32[2,1024]{1,0:T(2,128)S(1)}, s32[2,1024]{1,0:T(2,128)}, u32[]{:S(2)}) copy-start(s32[2,1024]{1,0:T(2,128)} %copy-done.28) | copy-start | bytes 24580 | tf_op jit(solution)/shard_map/while
  471.6 2.4 copy-start.28
  501.8 19.5 %copy-start.29 = (s32[2,1024]{1,0:T(2,128)S(1)}, s32[2,1024]{1,0:T(2,128)}, u32[]{:S(2)}) copy-start(s32[2,1024]{1,0:T(2,128)} %copy-done.28) | copy-start | bytes 24580 | tf_op jit(solution)/shard_map/while
  530.9 5.4 copy-start.14
  530.9 5.4 copy-start.16
  541.5 358.4 %all-reduce.13.cloned.1.call-start = ((), (), s32[]{:S(2)}) async-start(), calls=%async_computation.2 | async-start | bytes 14155776 | tf_op jit(solution)/shard_map/psum | solution.py:254
  541.5 7.1 copy-start.21
  541.5 7.1 copy-start.24
  541.5 11.5 %slice-start = ((s8[6291456]{0:T(1024)(128)(4,1)}), s8[4194304]{0:T(1024)(128)(4,1)S(1)}, s32[]{:S(2)}) async-start(s8[6291456]{0:T(1024)(128)(4,1)} %bitcast.220), calls=%async_computation.4 | async-start | bytes 8388608
  548.6 4.4 slice-start.1
  548.6 4.4 copy-start.12
  552.8 1.9 copy-start.5
  552.8 1.9 copy-start.33
  552.8 1.9 copy-start.37
  552.8 1.9 copy-start.51
  552.8 1.9 copy-start.65
  558.4 108.3 %copy-start.46 = (f32[768]{0:T(1024)S(1)}, f32[768]{0:T(1024)}, u32[]{:S(2)}) copy-start(f32[768]{0:T(1024)} %get-tuple-element.435) | copy-start | bytes 9220
  558.4 108.3 %copy-start.47 = (f32[768]{0:T(1024)S(1)}, f32[768]{0:T(1024)}, u32[]{:S(2)}) copy-start(f32[768]{0:T(1024)} %get-tuple-element.440) | copy-start | bytes 9220
  558.4 108.3 %copy-start.48 = (f32[768]{0:T(1024)S(1)}, f32[768]{0:T(1024)}, u32[]{:S(2)}) copy-start(f32[768]{0:T(1024)} %get-tuple-element.547) | copy-start | bytes 9220
  558.4 108.3 %copy-start.49 = (f32[768]{0:T(1024)S(1)}, f32[768]{0:T(1024)}, u32[]{:S(2)}) copy-start(f32[768]{0:T(1024)} %get-tuple-element.569) | copy-start | bytes 9220
  558.4 108.3 %copy-start.56 = (f32[768]{0:T(1024)S(1)}, f32[768]{0:T(1024)}, u32[]{:S(2)}) copy-start(f32[768]{0:T(1024)} %get-tuple-element.544) | copy-start | bytes 9220
  558.4 150.2 %copy-start.55 = (f32[768]{0:T(1024)S(1)}, f32[768]{0:T(1024)}, u32[]{:S(2)}) copy-start(f32[768]{0:T(1024)} %param.43) | copy-start | bytes 9220
  661.4 53.8 %slice-start.2 = ((s8[6291456]{0:T(1024)(128)(4,1)}), s8[2097152]{0:T(1024)(128)(4,1)S(1)}, s32[]{:S(2)}) async-start(s8[6291456]{0:T(1024)(128)(4,1)} %bitcast.222), calls=%async_computation.6 | async-start | bytes 4194304
  708.6 6.6 slice-start.3
  708.7 7.4 copy-start.6
  708.7 8.7 copy-start.10
  899.9 4.9 copy-start.26
  899.9 6.3 copy-start.25
  899.9 7.7 copy-start.1
  (21 other events, 23.9 us)
Sparse Core Ops, SparseCore 0:
  69.1 157.4 all-gather.2
  275.4 119.5 all-reduce.10
  541.6 119.8 all-reduce.14
  666.9 232.9 all-reduce.12
